TPU v7x, 32 devices: a whole 2x2x4 slice. The times are simulated.
32 devices in a mesh: groups: 2 (over y), dp: 4 (over z), mp: 4 (over x, core).
Axes of the slice: x: 2, y: 2, z: 4, core: 2. Of those that a mesh axis runs over, the one named last changes fastest.
Arguments:
- hidden: bfloat16 [8, 8192], P(('groups', 'mp'), 'dp'), parts along dimension 0, may hold values from -530 to 530
- attention_gain: float32 [8192], P('dp'), may hold values from 0.25 to 1.75
- query_weight: bfloat16 [8192, 8192], P('dp', 'mp'), may hold values from -0.0625 to 0.0625
- key_projector: bfloat16 [8192, 1024], P('dp', 'mp'), may hold values from -0.0625 to 0.0625
- value_projector: bfloat16 [8192, 1024], P('dp', 'mp'), may hold values from -0.0625 to 0.0625
- out_weight: bfloat16 [8192, 8192], P('mp', 'dp'), may hold values from -0.1875 to 0.1875
- key_cache: bfloat16 [8, 8, 256, 128], P(('groups', 'dp'), 'mp'), parts along dimension 0, may hold values from -1230 to 1230
- earlier_value_cache: bfloat16 [8, 8, 256, 128], P(('groups', 'dp'), 'mp'), parts along dimension 0, may hold values from -6 to 6
- cached_length_per_row: int32 [8], P(('groups', 'dp')), parts along dimension 0, may hold values from 1 to 256
- final_gain: float32 [8192], replicated, may hold values from 0.25 to 1.75
- head_weight: bfloat16 [32000, 8192], P('dp', 'mp'), may hold values from -41 to 41
- draft_ids: int32 [8], P(('groups', 'mp')), parts along dimension 0, may hold values from 0 to 31999
Outputs:
- residual_out: bfloat16 [8, 8192], P(('groups', 'mp'), 'dp'), parts along dimension 0
- draft_logprob: float32 [8], P(('groups', 'mp')), parts along dimension 0
There are 2 independent parts, one for each index of `groups`. A program takes and returns all parts, laid end to end along the dimension named above; an argument that names none is the same for every part. Nothing has to cross between parts.
All inputs are finite; a program needn't handle non-finite values.
Results may differ from a plain program's by a relative error of at most 0.0035.
Values may be sent and summed in bfloat16 or wider, within the bound.
A program may use at most 128 MiB of HBM per device.

v0:
```python
import functools
import math

import jax
import jax.numpy as jnp
from jax import lax
from jax.experimental import pallas as pl
from jax.experimental.pallas import tpu as pltpu
from jax.sharding import PartitionSpec as P

EPSILON = 1e-05
THETA = 10000.0
LANES = 128
MESH = pl.DeviceIdType.MESH
F32 = jnp.float32
BF16 = jnp.bfloat16


def each(first, last, body):
    if last - first <= 16:
        for k in range(first, last):
            body(k)
    else:

        @pl.loop(first, last)
        def _(k):
            body(k)


def aligned(start):
    return start if isinstance(start, int) else pl.multiple_of(start, LANES)


def kernel(
    n_dp, n_mp, chunk,
    hidden, attention_gain, query_weight, key_projector, value_projector, out_weight,
    key_cache, value_cache, lengths, final_gain, head_weight, draft_ids,
    residual_out, logprob_out,
    hid_v, gain_v, wq_v, wk_v, wv_v, wo_v, kc_v, vc_v, fgain_v, head_v,
    x_recv, x_v, ss_send, ss_recv, proj_send, proj_recv, mix_send, mix_recv, mix_v,
    att_send, att_recv, res_send, res_recv, ss2_send, ss2_recv, y_v,
    log_send, log_recv, fin_send, fin_recv,
    load_sem, head_sem, out_sem,
    x_ss, x_rs, ss_ss, ss_rs, proj_ss, proj_rs, mix_ss, mix_rs, att_ss, att_rs,
    res_ss, res_rs, ss2_ss, ss2_rs, log_ss, log_rs, fin_ss, fin_rs,
):
    j = lax.axis_index("dp")
    i = lax.axis_index("mp")
    count = n_dp * n_mp
    me = j * n_mp + i
    rows, width = hid_v.shape
    total_rows = rows * n_mp
    model_width = width * n_dp
    sequences, pairs, slots, head_size = kc_v.shape
    query_cols = wq_v.shape[1]
    pair_cols = wk_v.shape[1]
    group = query_cols // pair_cols
    quarter = y_v.shape[1]
    blocks = quarter // width
    vocab = head_v.shape[0]
    chunks = log_send.shape[0]
    full = vocab // chunk

    def load(source, target, slot):
        copy = pltpu.make_async_copy(source, target, load_sem.at[slot])
        copy.start()
        return copy

    hid_in = load(hidden, hid_v, 0)
    gain_in = load(attention_gain, gain_v, 1)
    wk_in = load(key_projector, wk_v, 2)
    wv_in = load(value_projector, wv_v, 3)
    wq_in = load(query_weight, wq_v, 4)
    kc_in = load(key_cache, kc_v, 5)
    vc_in = load(value_cache, vc_v, 6)
    wo_in = load(out_weight, wo_v, 7)
    fgain_in = load(final_gain.at[:, pl.ds(pl.multiple_of(i * quarter, LANES), quarter)], fgain_v, 8)

    def head_copy(c):
        size = chunk if c < full else vocab - full * chunk
        return pltpu.make_async_copy(
            head_weight.at[pl.ds(c * chunk, size)], head_v.at[pl.ds(c * chunk, size)], head_sem.at[c]
        )

    for c in range(chunks):
        head_copy(c).start()

    def place(number):
        return {"dp": number // n_mp, "mp": lax.rem(number, n_mp)}

    barrier = pltpu.get_barrier_semaphore()

    def greet(k):
        pl.semaphore_signal(
            barrier, inc=1, device_id=place(lax.rem(me + k, count)), device_id_type=MESH
        )

    each(1, count, greet)

    def remote(source, target, send, receive, device):
        return pltpu.make_async_remote_copy(
            src_ref=source, dst_ref=target, send_sem=send, recv_sem=receive,
            device_id=device, device_id_type=MESH,
        )

    hid_in.wait()
    own = hid_v[...].astype(F32)
    ss_send[...] = jnp.broadcast_to(jnp.sum(own * own, axis=1, keepdims=True), ss_send.shape)
    ss_recv[me] = ss_send[...]
    x_recv[i] = hid_v[...]

    lane = lax.broadcasted_iota(jnp.int32, (1, head_size), 1)
    half = head_size // 2
    index = jnp.where(lane < half, lane, lane - half).astype(F32)
    frequency = jnp.exp(index * (-2.0 * math.log(THETA) / head_size))
    turns = []
    for s in range(sequences):
        angles = lengths[s].astype(F32) * frequency
        sine = jnp.sin(angles)
        turns.append((jnp.cos(angles), jnp.where(lane < half, -sine, sine)))

    pl.semaphore_wait(barrier, count - 1)

    def x_copy(k):
        return remote(
            hid_v, x_recv.at[i], x_ss.at[k], x_rs.at[i], {"dp": j, "mp": lax.rem(i + k, n_mp)}
        )

    def ss_copy(k):
        return remote(
            ss_send, ss_recv.at[me], ss_ss.at[k], ss_rs.at[me], place(lax.rem(me + k, count))
        )

    each(1, count, lambda k: ss_copy(k).start())
    each(1, n_mp, lambda k: x_copy(k).start())

    def arrived(n, mine, buffer, sems):
        def one(k):
            source = lax.rem(mine + k, n)
            pltpu.make_async_copy(buffer.at[source], buffer.at[source], sems.at[source]).wait()

        each(1, n, one)

    def row_scales(buffer):
        scales = []
        for r in range(n_mp):
            squares = buffer[r]
            for d in range(1, n_dp):
                squares += buffer[d * n_mp + r]
            scales.append(lax.rsqrt(squares[:, :1] / model_width + EPSILON))
        return scales

    gain_in.wait()
    arrived(n_mp, i, x_recv, x_rs)
    arrived(count, me, ss_recv, ss_rs)
    scales = row_scales(ss_recv)
    gain = gain_v[...]
    x_v[...] = jnp.concatenate(
        [x_recv[r].astype(F32) * scales[r] * gain for r in range(n_mp)], axis=0
    ).astype(BF16)

    def project(left, weight, keep, base, parts, size):
        columns = weight.shape[1]
        step = min(512, columns)

        def one(c):
            start = aligned(c * step)
            part = jnp.dot(left[...], weight[:, pl.ds(start, step)], preferred_element_type=F32)
            for t in range(parts):
                keep[t, :, pl.ds(aligned(base + start), step)] = part[t * size : (t + 1) * size]

        if columns == step:
            one(0)
        else:

            @pl.loop(0, columns // step)
            def _(c):
                one(c)

    wk_in.wait()
    project(x_v, wk_v, proj_send, query_cols, n_dp, sequences)
    wv_in.wait()
    project(x_v, wv_v, proj_send, query_cols + pair_cols, n_dp, sequences)
    wq_in.wait()
    project(x_v, wq_v, proj_send, 0, n_dp, sequences)

    def proj_copy(k):
        t = lax.rem(j + k, n_dp)
        return remote(
            proj_send.at[t], proj_recv.at[j], proj_ss.at[k], proj_rs.at[j], {"dp": t, "mp": i}
        )

    each(1, n_dp, lambda k: proj_copy(k).start())
    kc_in.wait()
    vc_in.wait()
    arrived(n_dp, j, proj_recv, proj_rs)
    proj_recv[j] = proj_send[j]
    projected = proj_recv[0]
    for d in range(1, n_dp):
        projected += proj_recv[d]

    def rotated(vectors, turn):
        swapped = jnp.concatenate([vectors[:, half:], vectors[:, :half]], axis=1)
        return (vectors * turn[0] + swapped * turn[1]).astype(BF16)

    scale = head_size ** (-0.5)
    for s in range(sequences):
        def heads_of(start, number):
            return jnp.concatenate(
                [
                    projected[s : s + 1, start + h * head_size : start + (h + 1) * head_size]
                    for h in range(number)
                ],
                axis=0,
            )

        queries = rotated(heads_of(0, pairs * group), turns[s])
        keys = rotated(heads_of(query_cols, pairs), turns[s])
        values = heads_of(query_cols + pair_cols, pairs).astype(BF16)
        mixed = []
        for g in range(pairs):
            query = queries[g * group : (g + 1) * group]
            own_score = scale * jnp.sum(
                query.astype(F32) * keys[g : g + 1].astype(F32), axis=1, keepdims=True
            )
            scores = scale * lax.dot_general(
                query, kc_v[s, g], (((1,), (1,)), ((), ())), preferred_element_type=F32
            )
            spots = lax.broadcasted_iota(jnp.int32, scores.shape, 1)
            scores = jnp.where(spots < lengths[s], scores, -jnp.inf)
            highest = jnp.maximum(jnp.max(scores, axis=1, keepdims=True), own_score)
            exponent = jnp.exp(scores - highest)
            own_exp = jnp.exp(own_score - highest)
            denominator = jnp.sum(exponent, axis=1, keepdims=True) + own_exp
            numerator = jnp.dot(exponent.astype(BF16), vc_v[s, g], preferred_element_type=F32)
            numerator += own_exp.astype(BF16).astype(F32) * values[g : g + 1].astype(F32)
            mixed.append(numerator / denominator)
        mixed = [m[h : h + 1] for m in mixed for h in range(group)]
        mix_send[s : s + 1] = jnp.concatenate(mixed, axis=1).astype(BF16)

    def mix_copy(k):
        return remote(
            mix_send, mix_recv.at[j], mix_ss.at[k], mix_rs.at[j],
            {"dp": lax.rem(j + k, n_dp), "mp": i},
        )

    each(1, n_dp, lambda k: mix_copy(k).start())
    mix_recv[j] = mix_send[...]
    wo_in.wait()
    arrived(n_dp, j, mix_recv, mix_rs)
    mix_v[...] = jnp.concatenate(
        [mix_recv[d].astype(F32) for d in range(n_dp)], axis=0
    ).astype(BF16)
    project(mix_v, wo_v, att_send, 0, n_mp, rows)

    def att_copy(k):
        t = lax.rem(i + k, n_mp)
        return remote(
            att_send.at[t], att_recv.at[i], att_ss.at[k], att_rs.at[i], {"dp": j, "mp": t}
        )

    each(1, n_mp, lambda k: att_copy(k).start())
    att_recv[i] = att_send[i]
    arrived(n_mp, i, att_recv, att_rs)
    attended = att_recv[0]
    for r in range(1, n_mp):
        attended += att_recv[r]
    residual = (hid_v[...].astype(F32) + attended).astype(BF16)
    res_send[...] = residual
    wide = residual.astype(F32)
    ss2_send[...] = jnp.broadcast_to(jnp.sum(wide * wide, axis=1, keepdims=True), ss2_send.shape)

    reader = j // blocks
    spot = lax.rem(j, blocks) * n_mp + i

    def res_copy(k):
        return remote(
            res_send, res_recv.at[spot], res_ss.at[k], res_rs.at[spot],
            {"dp": lax.rem(j + k, n_dp), "mp": reader},
        )

    def ss2_copy(k):
        return remote(
            ss2_send, ss2_recv.at[me], ss2_ss.at[k], ss2_rs.at[me], place(lax.rem(me + k, count))
        )

    each(1, n_dp, lambda k: res_copy(k).start())

    @pl.when(reader != i)
    def _():
        res_copy(0).start()

    @pl.when(reader == i)
    def _():
        res_recv[spot] = residual

    each(1, count, lambda k: ss2_copy(k).start())
    ss2_recv[me] = ss2_send[...]
    result = pltpu.make_async_copy(res_send, residual_out, out_sem)
    result.start()

    def res_wait(k):
        source = (i * blocks + k // n_mp) * n_mp + lax.rem(k, n_mp)

        @pl.when(source != me)
        def _():
            pltpu.make_async_copy(res_recv.at[k], res_recv.at[k], res_rs.at[k]).wait()

    each(0, blocks * n_mp, res_wait)
    fgain_in.wait()
    arrived(count, me, ss2_recv, ss2_rs)
    scales = row_scales(ss2_recv)
    y_v[...] = jnp.concatenate(
        [
            jnp.concatenate([res_recv[b * n_mp + r].astype(F32) for b in range(blocks)], axis=1)
            * scales[r]
            * fgain_v[...]
            for r in range(n_mp)
        ],
        axis=0,
    ).astype(BF16)

    def log_copy(c, k):
        t = lax.rem(i + k, n_mp)
        return remote(
            log_send.at[c, t], log_recv.at[c, i], log_ss.at[c * n_mp + k], log_rs.at[c * n_mp + i],
            {"dp": j, "mp": t},
        )

    def head_chunk(c, size):
        piece = 256
        for p in range(0, size, piece):
            wide_piece = min(piece, size - p)
            part = lax.dot_general(
                y_v[...], head_v[pl.ds(c * chunk + p, wide_piece)],
                (((1,), (1,)), ((), ())), preferred_element_type=F32,
            )
            for t in range(n_mp):
                log_send[c, t, :, p : p + wide_piece] = part[t * rows : (t + 1) * rows]
        each(1, n_mp, lambda k: log_copy(c, k).start())

    if full:

        @pl.loop(0, full)
        def _(c):
            start = pl.multiple_of(c * chunk, chunk)
            pltpu.make_async_copy(
                head_weight.at[pl.ds(start, chunk)], head_v.at[pl.ds(start, chunk)], head_sem.at[c]
            ).wait()
            head_chunk(c, chunk)

    if chunks > full:
        rest = vocab - full * chunk
        head_copy(full).wait()
        log_send[full, :, :, rest // LANES * LANES :] = jnp.zeros(
            (n_mp, rows, chunk - rest // LANES * LANES), F32
        )
        head_chunk(full, rest)

    ids = jnp.zeros((rows, 1), jnp.int32)
    row_index = lax.broadcasted_iota(jnp.int32, (rows, 1), 0)
    for r in range(rows):
        ids = jnp.where(row_index == r, draft_ids[r], ids)
    column = lax.broadcasted_iota(jnp.int32, (rows, chunk), 1)
    pieces = []
    target = jnp.zeros((rows, chunk), F32)
    for c in range(chunks):
        logits = log_send[c, i]
        for k in range(1, n_mp):
            source = lax.rem(i + k, n_mp)
            pltpu.make_async_copy(
                log_recv.at[c, source], log_recv.at[c, source], log_rs.at[c * n_mp + source]
            ).wait()
            logits += log_recv[c, source]
        if c >= full:
            logits = jnp.where(column < vocab - c * chunk, logits, -jnp.inf)
        target = jnp.where(column + (c * chunk + j * vocab) == ids, logits, target)
        pieces.append(logits)
    if chunks > full:
        inside = ids < (j + 1) * vocab
        target = jnp.where(inside, target, 0.0)
    peak = pieces[0]
    for piece in pieces[1:]:
        peak = jnp.maximum(peak, piece)
    peak = jnp.max(peak, axis=1, keepdims=True)
    mass = jnp.exp(pieces[0] - peak)
    for piece in pieces[1:]:
        mass += jnp.exp(piece - peak)
    mass = jnp.sum(mass, axis=1, keepdims=True)
    target = jnp.sum(target, axis=1, keepdims=True)
    lanes = lax.broadcasted_iota(jnp.int32, (rows, LANES), 1)
    fin_send[...] = jnp.where(lanes == 0, peak, jnp.where(lanes == 1, mass, target))

    def fin_copy(k):
        return remote(
            fin_send, fin_recv.at[j], fin_ss.at[k], fin_rs.at[j],
            {"dp": lax.rem(j + k, n_dp), "mp": i},
        )

    each(1, n_dp, lambda k: fin_copy(k).start())
    fin_recv[j] = fin_send[...]

    each(1, count, lambda k: ss_copy(k).wait_send())
    each(1, n_mp, lambda k: x_copy(k).wait_send())
    each(1, n_dp, lambda k: proj_copy(k).wait_send())
    each(1, n_dp, lambda k: mix_copy(k).wait_send())
    each(1, n_mp, lambda k: att_copy(k).wait_send())
    each(1, n_dp, lambda k: res_copy(k).wait_send())

    @pl.when(reader != i)
    def _():
        res_copy(0).wait_send()

    each(1, count, lambda k: ss2_copy(k).wait_send())
    for c in range(chunks):
        each(1, n_mp, lambda k: log_copy(c, k).wait_send())
    result.wait()
    arrived(n_dp, j, fin_recv, fin_rs)
    each(1, n_dp, lambda k: fin_copy(k).wait_send())

    tiles = [fin_recv[d] for d in range(n_dp)]
    overall = tiles[0][:, 0:1]
    for tile in tiles[1:]:
        overall = jnp.maximum(overall, tile[:, 0:1])
    mass = jnp.zeros_like(overall)
    target = jnp.zeros_like(overall)
    for tile in tiles:
        mass += tile[:, 1:2] * jnp.exp(tile[:, 0:1] - overall)
        target += tile[:, 2:3]
    logprob = target - (overall + jnp.log(mass))
    for r in range(rows):
        logprob_out[r] = logprob[r, 0]


def solution(mesh):
    n_dp, n_mp = mesh.shape["dp"], mesh.shape["mp"]

    def shards(
        hidden, attention_gain, query_weight, key_projector, value_projector, out_weight,
        key_cache, earlier_value_cache, cached_length_per_row, final_gain, head_weight, draft_ids,
    ):
        rows, width = hidden.shape
        sequences = key_cache.shape[0]
        query_cols = query_weight.shape[1]
        wide = query_cols + key_projector.shape[1] + value_projector.shape[1]
        vocab, quarter = head_weight.shape
        count = n_dp * n_mp
        chunk = min(1024, -(-vocab // LANES) * LANES)
        chunks = -(-vocab // chunk)
        blocks = quarter // width
        vmem, dma = pltpu.VMEM, pltpu.SemaphoreType.DMA
        flat = (1, width)
        scratch = [
            vmem(hidden.shape, BF16), vmem(flat, F32),
            *[vmem(w.shape, BF16) for w in (query_weight, key_projector, value_projector, out_weight)],
            vmem(key_cache.shape, BF16), vmem(earlier_value_cache.shape, BF16),
            vmem((1, quarter), F32), vmem(head_weight.shape, BF16),
            vmem((n_mp, rows, width), BF16), vmem((n_mp * rows, width), BF16),
            vmem((rows, LANES), F32), vmem((count, rows, LANES), F32),
            vmem((n_dp, sequences, wide), F32), vmem((n_dp, sequences, wide), F32),
            vmem((sequences, query_cols), BF16), vmem((n_dp, sequences, query_cols), BF16),
            vmem((n_dp * sequences, query_cols), BF16),
            vmem((n_mp, rows, width), F32), vmem((n_mp, rows, width), F32),
            vmem((rows, width), BF16), vmem((blocks * n_mp, rows, width), BF16),
            vmem((rows, LANES), F32), vmem((count, rows, LANES), F32),
            vmem((n_mp * rows, quarter), BF16),
            vmem((chunks, n_mp, rows, chunk), F32), vmem((chunks, n_mp, rows, chunk), F32),
            vmem((rows, LANES), F32), vmem((n_dp, rows, LANES), F32),
            dma((9,)), dma((chunks,)), dma,
            dma((n_mp,)), dma((n_mp,)), dma((count,)), dma((count,)),
            dma((n_dp,)), dma((n_dp,)), dma((n_dp,)), dma((n_dp,)), dma((n_mp,)), dma((n_mp,)),
            dma((n_dp,)), dma((blocks * n_mp,)), dma((count,)), dma((count,)),
            dma((chunks * n_mp,)), dma((chunks * n_mp,)), dma((n_dp,)), dma((n_dp,)),
        ]
        anywhere = pl.BlockSpec(memory_space=pl.ANY)
        scalars = pl.BlockSpec(memory_space=pltpu.SMEM)
        return pl.pallas_call(
            functools.partial(kernel, n_dp, n_mp, chunk),
            out_shape=(
                jax.ShapeDtypeStruct(hidden.shape, BF16),
                jax.ShapeDtypeStruct(draft_ids.shape, F32),
            ),
            in_specs=[anywhere] * 8 + [scalars] + [anywhere] * 2 + [scalars],
            out_specs=(anywhere, scalars),
            scratch_shapes=scratch,
            compiler_params=pltpu.CompilerParams(
                collective_id=0, has_side_effects=True, vmem_limit_bytes=67043328
            ),
        )(
            hidden, attention_gain.reshape(flat), query_weight, key_projector, value_projector,
            out_weight, key_cache, earlier_value_cache, cached_length_per_row,
            final_gain.reshape(1, -1), head_weight, draft_ids,
        )

    in_specs = (
        P(("groups", "mp"), "dp"),
        P("dp"),
        P("dp", "mp"),
        P("dp", "mp"),
        P("dp", "mp"),
        P("mp", "dp"),
        P(("groups", "dp"), "mp", None, None),
        P(("groups", "dp"), "mp", None, None),
        P(("groups", "dp")),
        P(),
        P("dp", "mp"),
        P(("groups", "mp")),
    )
    out_specs = (P(("groups", "mp"), "dp"), P(("groups", "mp")))
    return jax.shard_map(shards, mesh=mesh, in_specs=in_specs, out_specs=out_specs, check_vma=False)
```

profile of v0, /device:TPU:0, one launch (start us, length us, event | category | flops | bytes accessed | tf_op | source)
XLA Modules:
  0.0 51.6 jit_solution(14738383383451280513)
XLA Ops:
  1.9 46.6 %shard_map.131 = (bf16[1,2048]{1,0:T(2,128)(2,1)}, f32[1]{0:T(128)}) custom-call(bf16[1,2048]{1,0:T(2,128)(2,1)} %hidden.1, f32[1,2048]{1,0:T(1,128)} %bitcast.3, bf16[2048,2048]{1,0:T(8,128)(2,1)} %query_weight.1, bf16[2048,256]{1,0:T(8,128)(2,1)} %key_projector.1, bf16[2048,256]{1,0:T(8,128)(2,1)} %value_projector.1, bf16[2048,2048]{1,0:T(8,128)(2,1)} %out_weight.1, ...), custom_call_target="tpu_custom_call" | custom-call | tf_op jit(solution)/shard_map/pallas_call | solution.py:477
  48.5 1.3 %copy.18 = bf16[1,2048]{1,0:T(2,128)(2,1)} copy(bf16[1,2048]{1,0:T(2,128)(2,1)} %get-tuple-element.4) | data formatting | bytes 8192
where the time goes:
time: 51.9 us; the launch traced here: 51.6 us
  Pallas kernels  46.6 us (90%)
  between operations  3.7 us (7%)
  local copies, waits for them, and re-layouts  1.3 us (3%)
    pallas_call x1, Pallas kernels, shards(): pl.pallas_call(functools.partial(kernel, n_dp, n_mp, chunk), out_shape=(j...  46.6 us
    unnamed x1, local copies, waits for them, and re-layouts  1.3 us

commit v1 on v0

v1 whole, which is shorter than its diff:
```python
import functools
import math

import jax
import jax.numpy as jnp
from jax import lax
from jax.experimental import pallas as pl
from jax.experimental.pallas import tpu as pltpu
from jax.sharding import PartitionSpec as P

EPSILON = 1e-05
THETA = 10000.0
LANES = 128
MESH = pl.DeviceIdType.MESH
F32 = jnp.float32
BF16 = jnp.bfloat16
WINDOWS = (2, 2, 1, 2)
REST_WINDOW = 2
VMEM_BYTES = 62 * 1024 * 1024


def each(first, last, body):
    if last - first <= 16:
        for k in range(first, last):
            body(k)
    else:

        @pl.loop(first, last)
        def _(k):
            body(k)


def aligned(start):
    return start if isinstance(start, int) else pl.multiple_of(start, LANES)


BLOCK = 256


def halves(columns):
    if columns % (4 * LANES):
        return [(0, columns)]
    return [(0, columns // 2), (columns // 2, columns // 2)]


def kernel(
    n_dp, n_mp, chunk, windows,
    hidden, attention_gain, query_weight, key_projector, value_projector, out_weight,
    key_cache, value_cache, lengths_in, final_gain, head_weight, ids_in,
    residual_out, logprob_out,
    hid_v, gain_v, wq_v, wk_v, wv_v, wo_v, kc_v, vc_v, fgain_v, head_v,
    x_recv, x_v, sum_send, sum_recv, proj_send, proj_recv, mix_send, mix_recv, mix_v,
    att_send, att_recv, own_send, own_recv, res_send, res_sent, res_recv, ss_send, ss_recv, y_v,
    log_send, log_recv, fin_send, fin_recv, lengths, draft_ids,
    load_sem, head_sem,
    x_ss, x_rs, sum_ss, sum_rs, proj_ss, proj_rs, mix_ss, mix_rs, att_ss, att_rs,
    own_ss, own_rs, res_ss, res_rs, ss_ss, ss_rs, log_ss, log_rs, fin_ss, fin_rs,
):
    j = lax.axis_index("dp")
    i = lax.axis_index("mp")
    count = n_dp * n_mp
    me = j * n_mp + i
    rows, width = hid_v.shape
    model_width = width * n_dp
    sequences, pairs, slots, head_size = kc_v.shape
    query_cols = wq_v.shape[1]
    pair_cols = wk_v.shape[1]
    group = query_cols // pair_cols
    quarter = y_v.shape[1]
    blocks = quarter // width
    vocab = head_v.shape[0]
    chunks = log_send.shape[0]
    full = vocab // chunk
    rest = vocab - full * chunk
    even = chunk % BLOCK == 0 and quarter % BLOCK == 0
    plan = []
    for w, number in enumerate(windows):
        first = sum(windows[:w])
        mine = [c for c in range(first, first + number) if c < full]
        if w == REST_WINDOW and rest >= BLOCK:
            mine.append(full)
        plan.append(mine if even else [])
    order = [c for mine in plan for c in mine]
    turned = set(order)
    order += [c for c in range(chunks) if c not in turned]

    far_half = j // ((n_dp + 1) // 2)
    reach = jnp.maximum(j, n_dp - 1 - j)

    def far(k):
        step = (k - 1) + (k - 1) // reach
        return far_half * step + (1 - far_half) * (n_dp - 1 - step)

    def everyone(action):
        def along(k):
            for step in range(n_mp):
                action(far(k), lax.rem(i + step, n_mp))

        each(1, n_dp, along)
        for step in range(1, n_mp):
            action(j, lax.rem(i + step, n_mp))

    def load(source, target, slot):
        copy = pltpu.make_async_copy(source, target, load_sem.at[slot])
        copy.start()
        return copy

    hid_in = load(hidden, hid_v, 0)
    barrier = pltpu.get_barrier_semaphore()
    everyone(
        lambda dp, mp: pl.semaphore_signal(
            barrier, inc=1, device_id={"dp": dp, "mp": mp}, device_id_type=MESH
        )
    )

    gain_in = load(attention_gain, gain_v, 1)
    len_in = load(lengths_in, lengths, 9)
    ids_load = load(ids_in, draft_ids, 10)
    wk_in = load(key_projector, wk_v, 2)
    wv_in = load(value_projector, wv_v, 3)
    wq_in = load(query_weight, wq_v, 4)
    kc_in = load(key_cache, kc_v, 5)
    vc_in = load(value_cache, vc_v, 6)

    def head_copy(c):
        size = chunk if c < full else vocab - full * chunk
        return pltpu.make_async_copy(
            head_weight.at[pl.ds(c * chunk, size)], head_v.at[pl.ds(c * chunk, size)], head_sem.at[c]
        )

    def remote(source, target, send, receive, device):
        return pltpu.make_async_remote_copy(
            src_ref=source, dst_ref=target, send_sem=send, recv_sem=receive,
            device_id=device, device_id_type=MESH,
        )

    def x_copy(k):
        return remote(
            hid_v, x_recv.at[i], x_ss, x_rs, {"dp": j, "mp": lax.rem(i + k, n_mp)}
        )

    def finished(copies, buffer, sem):
        if copies:
            pltpu.make_async_copy(
                buffer.at[pl.ds(0, copies)], buffer.at[pl.ds(0, copies)], sem
            ).wait()

    def sum_copy(dp, mp):
        return remote(
            sum_send, sum_recv.at[me], sum_ss, sum_rs, {"dp": dp, "mp": mp}
        )

    hid_in.wait()
    own = hid_v[...].astype(F32)
    sum_send[...] = jnp.broadcast_to(jnp.sum(own * own, axis=1, keepdims=True), sum_send.shape)
    sum_recv[me] = sum_send[...]
    x_recv[i] = hid_v[...]
    pl.semaphore_wait(barrier, count - 1)
    everyone(lambda dp, mp: sum_copy(dp, mp).start())
    each(1, n_mp, lambda k: x_copy(k).start())
    wo_in = load(out_weight, wo_v, 7)
    len_in.wait()
    lane = lax.broadcasted_iota(jnp.int32, (1, head_size), 1)
    half = head_size // 2
    index = jnp.where(lane < half, lane, lane - half).astype(F32)
    frequency = jnp.exp(index * (-2.0 * math.log(THETA) / head_size))
    turns = []
    for s in range(sequences):
        angles = lengths[s].astype(F32) * frequency
        sine = jnp.sin(angles)
        turns.append((jnp.cos(angles), jnp.where(lane < half, -sine, sine)))
    gain_in.wait()
    gain = gain_v[...]

    def scale_of(squares):
        return lax.rsqrt(squares / model_width + EPSILON)

    finished(n_mp - 1, x_recv, x_rs)
    for c in order[:3]:
        head_copy(c).start()
    wk_in.wait()
    wv_in.wait()
    wq_in.wait()
    finished(count - 1, sum_recv, sum_rs)
    normed = []
    for r in range(n_mp):
        squares = sum_recv[r]
        for d in range(1, n_dp):
            squares += sum_recv[d * n_mp + r]
        normed.append(x_recv[r].astype(F32) * scale_of(squares[:, :1]) * gain)
    x_v[...] = jnp.concatenate(normed, axis=0).astype(BF16)

    def proj_copy(k, start, size):
        t = far(k)
        lanes = pl.ds(start, size)
        return remote(
            proj_send.at[t, :, lanes], proj_recv.at[j, :, lanes], proj_ss, proj_rs,
            {"dp": t, "mp": i},
        )

    def proj_out(parts):
        first = parts[0][0]
        last = first
        for start, part in parts:
            last = start + part.shape[1]
            for t in range(n_dp):
                proj_send[t, :, start:last] = part[t * sequences : (t + 1) * sequences]
        each(1, n_dp, lambda k: proj_copy(k, first, last - first).start())

    def piece(left, weight, start, size):
        return jnp.dot(left[...], weight[:, start : start + size], preferred_element_type=F32)

    held = None
    for start, size in halves(query_cols):
        part = piece(x_v, wq_v, start, size)
        if held is not None:
            proj_out(held)
        held = [(start, part)]
    tail = [
        (query_cols, piece(x_v, wk_v, 0, pair_cols)),
        (query_cols + pair_cols, piece(x_v, wv_v, 0, pair_cols)),
    ]
    proj_out(held)
    proj_out(tail)
    fgain_in = load(
        final_gain.at[:, pl.ds(pl.multiple_of(i * quarter, LANES), quarter)], fgain_v, 8
    )
    for c in order[3:]:
        head_copy(c).start()
    kc_in.wait()
    vc_in.wait()
    proj_recv[j] = proj_send[j]

    def turn(start, blocks):
        for p in range(0, blocks * BLOCK, BLOCK):
            for k in range(0, quarter, BLOCK):
                spot = (pl.ds(start + p, BLOCK), slice(k, k + BLOCK))
                head_v[spot] = head_v[spot].T

    def use_window(w):
        for c in plan[w]:
            head_copy(c).wait()
            turn(c * chunk, (chunk if c < full else rest) // BLOCK)

    use_window(0)
    finished(n_dp - 1, proj_recv, proj_rs)
    projected = proj_recv[0]
    for d in range(1, n_dp):
        projected += proj_recv[d]

    def rotated(vectors, turn):
        swapped = jnp.concatenate([vectors[:, half:], vectors[:, :half]], axis=1)
        return (vectors * turn[0] + swapped * turn[1]).astype(BF16)

    scale = head_size ** (-0.5)
    for s in range(sequences):
        def heads_of(start, number):
            return jnp.concatenate(
                [
                    projected[s : s + 1, start + h * head_size : start + (h + 1) * head_size]
                    for h in range(number)
                ],
                axis=0,
            )

        queries = rotated(heads_of(0, pairs * group), turns[s])
        keys = rotated(heads_of(query_cols, pairs), turns[s])
        values = heads_of(query_cols + pair_cols, pairs).astype(BF16)
        mixed = []
        for g in range(pairs):
            query = queries[g * group : (g + 1) * group]
            own_score = scale * jnp.sum(
                query.astype(F32) * keys[g : g + 1].astype(F32), axis=1, keepdims=True
            )
            scores = scale * lax.dot_general(
                query, kc_v[s, g], (((1,), (1,)), ((), ())), preferred_element_type=F32
            )
            spots = lax.broadcasted_iota(jnp.int32, scores.shape, 1)
            scores = jnp.where(spots < lengths[s], scores, -jnp.inf)
            highest = jnp.maximum(jnp.max(scores, axis=1, keepdims=True), own_score)
            exponent = jnp.exp(scores - highest)
            own_exp = jnp.exp(own_score - highest)
            denominator = jnp.sum(exponent, axis=1, keepdims=True) + own_exp
            numerator = jnp.dot(exponent.astype(BF16), vc_v[s, g], preferred_element_type=F32)
            numerator += own_exp.astype(BF16).astype(F32) * values[g : g + 1].astype(F32)
            mixed.append(numerator / denominator)
        mixed = [m[h : h + 1] for m in mixed for h in range(group)]
        mix_send[s : s + 1] = jnp.concatenate(mixed, axis=1).astype(BF16)

    def mix_copy(k):
        return remote(
            mix_send, mix_recv.at[j], mix_ss, mix_rs, {"dp": far(k), "mp": i},
        )

    each(1, n_dp, lambda k: mix_copy(k).start())
    mix_recv[j] = mix_send[...]
    wo_in.wait()
    use_window(1)
    finished(n_dp - 1, mix_recv, mix_rs)
    mix_v[...] = jnp.concatenate(
        [mix_recv[d].astype(F32) for d in range(n_dp)], axis=0
    ).astype(BF16)

    reader = j // blocks
    spot = lax.rem(j, blocks)

    def att_copy(start, size):
        lanes = pl.ds(start, size)
        return remote(
            att_send.at[:, lanes], att_recv.at[i, :, lanes], att_ss, att_rs,
            {"dp": j, "mp": reader},
        )

    def att_out(start, part):
        size = part.shape[1]
        att_send[:, start : start + size] = part

        @pl.when(reader != i)
        def _():
            att_copy(start, size).start()

    held = None
    for start, size in halves(width):
        part = piece(mix_v, wo_v, start, size)
        if held is not None:
            att_out(*held)
        held = (start, part)
    att_out(*held)
    use_window(2)

    def res_copy(dp):
        return remote(res_send, res_recv.at[spot], res_ss, res_rs, {"dp": dp, "mp": i})

    def own_copy(k):
        t = lax.rem(i + k, n_mp)
        return remote(own_send.at[t], own_recv, own_ss, own_rs, {"dp": j, "mp": t})

    @pl.when(reader == i)
    def _():
        attended = att_send[...] + jnp.concatenate(
            [x_recv[r].astype(F32) for r in range(n_mp)], axis=0
        )
        finished(n_mp - 1, att_recv, att_rs)
        for k in range(1, n_mp):
            attended += att_recv[lax.rem(i + k, n_mp)]
        residual = attended.astype(BF16)
        res_send[...] = residual
        each(1, n_dp, lambda k: res_copy(far(k)).start())
        res_recv[spot] = residual
        for r in range(n_mp):
            own_send[r] = residual[r * rows : (r + 1) * rows]
        each(1, n_mp, lambda k: own_copy(k).start())
        residual_out[...] = own_send[i]

    ids_load.wait()
    ids = jnp.zeros((rows, 1), jnp.int32)
    row_index = lax.broadcasted_iota(jnp.int32, (rows, 1), 0)
    for r in range(rows):
        ids = jnp.where(row_index == r, draft_ids[r], ids)
    fgain_in.wait()
    final = fgain_v[...]
    use_window(3)

    @pl.when(reader == i)
    def _():
        finished(blocks - 1, res_recv, res_rs)

    @pl.when(reader != i)
    def _():
        finished(blocks, res_recv, res_rs)

    wides = jnp.concatenate([res_recv[b].astype(F32) for b in range(blocks)], axis=1)
    y_v[...] = (wides * final).astype(BF16)
    squares = jnp.sum(wides * wides, axis=1, keepdims=True)
    for r in range(n_mp):
        ss_send[r] = jnp.broadcast_to(squares[r * rows : (r + 1) * rows], (rows, LANES))

    def ss_copy(k):
        t = lax.rem(i + k, n_mp)
        return remote(ss_send.at[t], ss_recv.at[i], ss_ss, ss_rs, {"dp": j, "mp": t})

    def log_copy(c, k):
        t = lax.rem(i + k, n_mp)
        return remote(
            log_send.at[c, t], log_recv.at[c, i], log_ss.at[c], log_rs.at[c],
            {"dp": j, "mp": t},
        )

    def keep_logits(c, parts):
        for p, part in parts:
            for t in range(n_mp):
                log_send[c, t, :, p : p + part.shape[1]] = part[t * rows : (t + 1) * rows]

    def head_chunk(c):
        size = chunk if c < full else rest
        ready = size // BLOCK * BLOCK if c in turned else 0
        if c not in turned:
            head_copy(c).wait()
        parts = []
        for p in range(0, ready, BLOCK):
            part = None
            for k in range(0, quarter, BLOCK):
                one = jnp.dot(
                    y_v[:, k : k + BLOCK], head_v[pl.ds(c * chunk + p, BLOCK), k : k + BLOCK],
                    preferred_element_type=F32,
                )
                part = one if part is None else part + one
            parts.append((p, part))
        for p in range(ready, size, BLOCK):
            part = lax.dot_general(
                y_v[...], head_v[pl.ds(c * chunk + p, min(BLOCK, size - p))],
                (((1,), (1,)), ((), ())), preferred_element_type=F32,
            )
            parts.append((p, part))
        return parts

    each(1, n_mp, lambda k: ss_copy(k).start())
    if rest:
        log_send[full, :, :, rest // LANES * LANES :] = jnp.zeros(
            (n_mp, rows, chunk - rest // LANES * LANES), F32
        )
    for at, c in enumerate(order):
        parts = head_chunk(c)
        if at:
            each(1, n_mp, lambda k: log_copy(order[at - 1], k).start())
        keep_logits(c, parts)
    each(1, n_mp, lambda k: log_copy(order[-1], k).start())

    finished(n_mp - 1, ss_recv, ss_rs)
    squares = ss_send[i]
    for k in range(1, n_mp):
        squares += ss_recv[lax.rem(i + k, n_mp)]
    scales = scale_of(squares[:, :1])
    column = lax.broadcasted_iota(jnp.int32, (rows, chunk), 1)

    def stats(group):
        pieces, target, peak = [], jnp.zeros((rows, chunk), F32), None
        for c in group:
            logits = log_send[c, i]
            finished(n_mp - 1, log_recv.at[c], log_rs.at[c])
            for k in range(1, n_mp):
                logits += log_recv[c, lax.rem(i + k, n_mp)]
            logits = logits * scales
            here = ids - (c * chunk + j * vocab)
            if c >= full:
                logits = jnp.where(column < rest, logits, -jnp.inf)
                here = jnp.where(here < rest, here, -1)
            target = jnp.where(column == here, logits, target)
            pieces.append(logits)
            peak = logits if peak is None else jnp.maximum(peak, logits)
        peak = jnp.max(peak, axis=1, keepdims=True)
        mass = sum(jnp.exp(piece - peak) for piece in pieces)
        return peak, jnp.sum(mass, axis=1, keepdims=True), jnp.sum(target, axis=1, keepdims=True)

    early = stats(order[:-1]) if chunks > 1 else None
    peak, mass, target = stats(order[-1:])
    if early is not None:
        early_peak, early_mass, early_target = early
        top = jnp.maximum(peak, early_peak)
        mass = mass * jnp.exp(peak - top) + early_mass * jnp.exp(early_peak - top)
        peak, target = top, target + early_target
    for p, value in enumerate((peak, mass, target)):
        fin_send[p] = jnp.broadcast_to(value, (rows, LANES))

    def fin_copy(k):
        return remote(
            fin_send, fin_recv.at[j], fin_ss, fin_rs,
            {"dp": far(k), "mp": i},
        )

    each(1, n_dp, lambda k: fin_copy(k).start())
    fin_recv[j] = fin_send[...]

    finished(n_mp - 1, x_recv, x_ss)
    finished(count - 1, sum_recv, sum_ss)
    finished(n_dp - 1, proj_recv, proj_ss)
    finished(n_dp - 1, mix_recv, mix_ss)

    @pl.when(reader == i)
    def _():
        finished(n_dp - 1, res_sent, res_ss)
        finished(n_mp - 1, own_send, own_ss)

    @pl.when(reader != i)
    def _():
        pltpu.make_async_copy(att_send, att_send, att_ss).wait()
        pltpu.make_async_copy(own_recv, own_recv, own_rs).wait()
        residual_out[...] = own_recv[...]

    finished(n_mp - 1, ss_recv, ss_ss)
    for c in range(chunks):
        finished(n_mp - 1, log_recv.at[c], log_ss.at[c])
    finished(n_dp - 1, fin_recv, fin_rs)
    finished(n_dp - 1, fin_recv, fin_ss)

    tiles = [fin_recv[d] for d in range(n_dp)]
    overall = tiles[0][0]
    for tile in tiles[1:]:
        overall = jnp.maximum(overall, tile[0])
    mass = jnp.zeros_like(overall)
    target = jnp.zeros_like(overall)
    for tile in tiles:
        mass += tile[1] * jnp.exp(tile[0] - overall)
        target += tile[2]
    logprob_out[...] = target - (overall + jnp.log(mass))


def deliver(residual, logprob, residual_out, logprob_out):
    residual_out[...] = residual[...]
    for r in range(logprob.shape[0]):
        logprob_out[r] = logprob[r, 0]


def solution(mesh):
    n_dp, n_mp = mesh.shape["dp"], mesh.shape["mp"]

    def shards(
        hidden, attention_gain, query_weight, key_projector, value_projector, out_weight,
        key_cache, earlier_value_cache, cached_length_per_row, final_gain, head_weight, draft_ids,
    ):
        rows, width = hidden.shape
        sequences = key_cache.shape[0]
        query_cols = query_weight.shape[1]
        wide = query_cols + key_projector.shape[1] + value_projector.shape[1]
        vocab, quarter = head_weight.shape
        chunk = min(1024, -(-vocab // LANES) * LANES)
        chunks = -(-vocab // chunk)
        blocks = quarter // width
        count = n_dp * n_mp
        vmem, dma, smem = pltpu.VMEM, pltpu.SemaphoreType.DMA, pltpu.SMEM
        flat = (1, width)
        scratch = [
            vmem(hidden.shape, BF16), vmem(flat, F32),
            *[vmem(w.shape, BF16) for w in (query_weight, key_projector, value_projector, out_weight)],
            vmem(key_cache.shape, BF16), vmem(earlier_value_cache.shape, BF16),
            vmem((1, quarter), F32), vmem(head_weight.shape, BF16),
            vmem((n_mp, rows, width), BF16), vmem((n_mp * rows, width), BF16),
            vmem((rows, LANES), F32), vmem((count, rows, LANES), F32),
            vmem((n_dp, sequences, wide), F32), vmem((n_dp, sequences, wide), F32),
            vmem((sequences, query_cols), BF16), vmem((n_dp, sequences, query_cols), BF16),
            vmem((n_dp * sequences, query_cols), BF16),
            vmem((n_mp * rows, width), F32), vmem((n_mp, n_mp * rows, width), F32),
            vmem((n_mp, rows, width), BF16), vmem((rows, width), BF16),
            vmem((n_mp * rows, width), BF16), vmem((n_dp, n_mp * rows, width), BF16),
            vmem((blocks, n_mp * rows, width), BF16),
            vmem((n_mp, rows, LANES), F32), vmem((n_mp, rows, LANES), F32),
            vmem((n_mp * rows, quarter), BF16),
            vmem((chunks, n_mp, rows, chunk), F32), vmem((chunks, n_mp, rows, chunk), F32),
            vmem((3, rows, LANES), F32), vmem((n_dp, 3, rows, LANES), F32),
            smem(cached_length_per_row.shape, jnp.int32), smem(draft_ids.shape, jnp.int32),
            dma((11,)), dma((chunks,)),
            *[dma] * 16, dma((chunks,)), dma((chunks,)), dma, dma,
        ]
        anywhere = pl.BlockSpec(memory_space=pl.ANY)
        far = pl.BlockSpec(memory_space=pltpu.HBM)
        inside = pl.BlockSpec(memory_space=pltpu.VMEM)
        scalars = pl.BlockSpec(memory_space=pltpu.SMEM)
        residual, logprob = pl.pallas_call(
            functools.partial(kernel, n_dp, n_mp, chunk, WINDOWS),
            out_shape=(vmem(hidden.shape, BF16), vmem((rows, LANES), F32)),
            in_specs=[anywhere] * 8 + [far] + [anywhere] * 2 + [far],
            out_specs=(inside, inside),
            scratch_shapes=scratch,
            compiler_params=pltpu.CompilerParams(
                collective_id=0, has_side_effects=True, vmem_limit_bytes=VMEM_BYTES
            ),
        )(
            hidden, attention_gain.reshape(flat), query_weight, key_projector, value_projector,
            out_weight, key_cache, earlier_value_cache, cached_length_per_row,
            final_gain.reshape(1, -1), head_weight, draft_ids,
        )
        return pl.pallas_call(
            deliver,
            out_shape=(
                jax.ShapeDtypeStruct(hidden.shape, BF16),
                jax.ShapeDtypeStruct(draft_ids.shape, F32),
            ),
            in_specs=[inside, inside],
            out_specs=(inside, scalars),
        )(
            pltpu.with_memory_space_constraint(residual, vmem),
            pltpu.with_memory_space_constraint(logprob, vmem),
        )

    in_specs = (
        P(("groups", "mp"), "dp"),
        P("dp"),
        P("dp", "mp"),
        P("dp", "mp"),
        P("dp", "mp"),
        P("mp", "dp"),
        P(("groups", "dp"), "mp", None, None),
        P(("groups", "dp"), "mp", None, None),
        P(("groups", "dp")),
        P(),
        P("dp", "mp"),
        P(("groups", "mp")),
    )
    out_specs = (P(("groups", "mp"), "dp"), P(("groups", "mp")))
    return jax.shard_map(shards, mesh=mesh, in_specs=in_specs, out_specs=out_specs, check_vma=False)
```

time: 51.9 us -> 40 us (0.77)
  Pallas kernels: 46.6 us -> 37.6 us
  between operations: 3.7 us -> 2.09 us
  local copies, waits for them, and re-layouts: 1.3 us -> 0 us
    pallas_call x1 -> x2, Pallas kernels: 46.6 us -> 37.6 us  [the longest x1 37 us: shards(): pl.pallas_call(functools.partial(kernel, n_dp, n_mp, chunk, WINDOWS), out...]
    unnamed x1 -> x0, local copies, waits for them, and re-layouts: 1.3 us -> none
where the time goes in v1:
time: 40 us; the launch traced here: 39.7 us
  Pallas kernels  37.6 us (94%)
  between operations  2.09 us (5%)
    pallas_call x1, Pallas kernels, shards(): pl.pallas_call(functools.partial(kernel, n_dp, n_mp, chunk, WINDOWS), out...  37 us

profile of v1, /device:TPU:0, one launch (start us, length us, event | category | flops | bytes accessed | tf_op | source)
XLA Modules:
  0.0 39.7 jit_solution(5466342488707896161)
XLA Ops:
  1.9 37.0 %shard_map.131 = (bf16[1,2048]{1,0:T(2,128)(2,1)S(1)}, f32[1,128]{1,0:T(1,128)S(1)}) custom-call(bf16[1,2048]{1,0:T(2,128)(2,1)} %hidden.1, f32[1,2048]{1,0:T(1,128)} %bitcast.3, bf16[2048,2048]{1,0:T(8,128)(2,1)} %query_weight.1, bf16[2048,256]{1,0:T(8,128)(2,1)} %key_projector.1, bf16[2048,256]{1,0:T(8,128)(2,1)} %value_projector.1, ...), custom_call_target="tpu_custom_call" | custom-call | tf_op jit(solution)/shard_map/pallas_call | solution.py:558
  38.9 0.6 %shard_map.132 = (bf16[1,2048]{1,0:T(2,128)(2,1)}, f32[1]{0:T(128)}) custom-call(bf16[1,2048]{1,0:T(2,128)(2,1)S(1)} %get-tuple-element.4.residual, f32[1,128]{1,0:T(1,128)S(1)} %get-tuple-element.5.logprob), custom_call_target="tpu_custom_call" | custom-call | tf_op jit(solution)/shard_map/pallas_call | solution.py:572
